TPU v7x, 32 devices: a whole 2x2x4 slice. The times are simulated.
32 devices in a mesh: lat: 2 (over x), lon: 4 (over y, core), lev: 4 (over z).
Axes of the slice: x: 2, y: 2, z: 4, core: 2. Of those that a mesh axis runs over, the one named last changes fastest.
Arguments:
- initial_state: float32 [16, 128, 256, 128], P('lat', 'lon', 'lev'), may hold values from 0.2 to 1.8
- scaled_diffusivity: float32 [16, 128, 256, 128], P('lat', 'lon', 'lev'), may hold values from 0.03 to 0.15
- scaled_forcing: float32 [16, 128, 256, 128], P('lat', 'lon', 'lev'), may hold values from -0.2 to 0.2
Outputs:
- cumulative_totals: float32 [16, 128, 256, 128], P('lat', 'lon', 'lev')
- temperature_end: float32 [16, 128, 256, 128], P('lat', 'lon', 'lev')
All inputs are finite; a program needn't handle non-finite values.
Results may differ from a plain program's by a relative error of at most 0.00002.
Values sent between devices are 32-bit elements; how exact they have to be, the bound alone decides.
A program may use at most 128 MiB of HBM per device.

v0:
```python
import jax
import jax.numpy as jnp
from jax import lax
from jax.sharding import PartitionSpec as P

STEPS = 4


def extended(block, sides, width):
    for axis, dim in sides:
        count = lax.axis_size(axis)
        forward = [(i, i + 1) for i in range(count - 1)]
        backward = [(target, source) for source, target in forward]
        low = lax.ppermute(
            lax.slice_in_dim(block, block.shape[dim] - width, None, axis=dim), axis, forward
        )
        high = lax.ppermute(lax.slice_in_dim(block, 0, width, axis=dim), axis, backward)
        block = jnp.concatenate([low, block, high], axis=dim)
    return block


def prefix(value, axis, join, neutral):
    count, mine = (lax.axis_size(axis), lax.axis_index(axis))
    pieces = lax.all_gather(value, axis)
    total = jnp.full_like(value, 0) + jnp.asarray(neutral, value.dtype)

    def lap(position, total):
        longer = join(total, pieces[position])
        return jnp.where(position < mine, longer, total)

    return lax.fori_loop(0, count - 1, lap, total)


def strip_edges(values, dims):
    for dim in dims:
        values = lax.slice_in_dim(values, 1, values.shape[dim] - 1, axis=dim)
    return values


def neighbour(values, dim, start, dims):
    others = [other for other in dims if other != dim]
    values = strip_edges(values, others)
    return lax.slice_in_dim(values, start, start + values.shape[dim] - 2, axis=dim)


def explicit_update(haloed_values, scaled_diffusivity, scaled_forcing):
    middle = strip_edges(haloed_values, (0, 1, 2))
    lower = [neighbour(haloed_values, dim, 0, (0, 1, 2)) for dim in (0, 1, 2)]
    upper = [neighbour(haloed_values, dim, 2, (0, 1, 2)) for dim in (0, 1, 2)]
    spread = lower[0] + upper[0] + lower[1] + upper[1] + lower[2] + upper[2] - 6.0 * middle
    return middle + scaled_diffusivity * spread + scaled_forcing


def per_device(initial_state, scaled_diffusivity, scaled_forcing):
    for step in range(STEPS):
        haloed_values = extended(initial_state, (("lat", 0), ("lon", 1), ("lev", 2)), 1)
        initial_state = explicit_update(haloed_values, scaled_diffusivity, scaled_forcing)
    present_layer = jnp.cumsum(initial_state, axis=1)
    total = lax.slice_in_dim(
        present_layer, present_layer.shape[1] - 1, present_layer.shape[1], axis=1
    )

    def add_pair(earlier_total, later_total):
        return earlier_total + later_total

    previous_plane = prefix(total, "lon", add_pair, jnp.zeros_like(total))
    cumulative_totals = (present_layer + previous_plane) / (
        initial_state.shape[1] * lax.axis_size("lon")
    )
    return (cumulative_totals, initial_state)


def solution(mesh):
    in_specs = (
        P("lat", "lon", "lev", None),
        P("lat", "lon", "lev", None),
        P("lat", "lon", "lev", None),
    )
    out_specs = (P("lat", "lon", "lev", None), P("lat", "lon", "lev", None))
    return jax.shard_map(
        per_device, mesh=mesh, in_specs=in_specs, out_specs=out_specs, check_vma=False
    )
```

profile of v0, /device:TPU:0, one launch (start us, length us, event | category | flops | bytes accessed | tf_op | source)
XLA Modules:
  0.0 376.7 jit_solution(261048938056370886)
XLA Ops:
  8.9 4.9 %collective-permute-start = (f32[1,32,64,128]{3,2,1,0:T(8,128)S(1)}, f32[1,32,64,128]{3,2,1,0:T(8,128)S(1)}, u32[]{:S(2)}, u32[]{:S(2)}) collective-permute-start(f32[1,32,64,128]{3,2,1,0:T(8,128)S(1)} %get-tuple-element.142), channel_id=1, source_target_pairs={{0,16},{1,17},{2,18},{3,19},{4,20},{5,21},{6,22},{7,23},{8,24},{9,... | collective-permute-start | bytes 3145736 | tf_op jit(solution)/shard_map/ppermute | solution.py:14
  15.1 21.0 %collective-permute-done = f32[1,32,64,128]{3,2,1,0:T(8,128)S(1)} collective-permute-done((f32[1,32,64,128]{3,2,1,0:T(8,128)S(1)}, f32[1,32,64,128]{3,2,1,0:T(8,128)S(1)}, u32[]{:S(2)}, u32[]{:S(2)}) %collective-permute-start) | collective-permute-done | bytes 1048608 | tf_op jit(solution)/shard_map/ppermute | solution.py:14
  36.2 4.2 %constant_dynamic-update-slice_fusion.1 = f32[10,32,64,128]{3,2,1,0:T(8,128)S(1)} fusion(f32[10,32,64,128]{3,2,1,0:T(8,128)S(1)} %constant_dynamic-update-slice_fusion.2, f32[8,32,64,128]{3,2,1,0:T(8,128)} %param.5), kind=kLoop, calls=%fused_computation.130 | loop fusion | bytes 16777216
  43.3 3.9 %collective-permute-done.3 = f32[10,1,64,128]{3,2,1,0:T(8,128)S(1)} collective-permute-done((f32[10,1,64,128]{3,2,1,0:T(8,128)S(1)}, f32[10,1,64,128]{3,2,1,0:T(8,128)S(1)}, u32[]{:S(2)}, u32[]{:S(2)}) %collective-permute-start.3) | collective-permute-done | bytes 327712 | tf_op jit(solution)/shard_map/ppermute | solution.py:17
  59.6 30.8 %fusion.31 = f32[8,32,64,128]{3,2,1,0:T(8,128)S(1)} fusion(f32[8,32,64,128]{3,2,1,0:T(8,128)} %param.7, f32[8,32,64,128]{3,2,1,0:T(8,128)} %param.5, f32[8,32,64,128]{3,2,1,0:T(8,128)} %param.6, f32[10,34,1,128]{3,2,1,0:T(1,128)} %copy.27, f32[10,1,64,128]{3,2,1,0:T(8,128)} %copy-done.4, f32[10,32,64,128]{3,2,1,0:T(8,128)} %copy-done.1, ...), kind=kLoop, calls=%fused_computation.87 | loop fusion | flops 41943040 | bytes 47140864 | tf_op jit(solution)/shard_map/add | solution.py:51
  90.5 4.5 %collective-permute-start.6 = (f32[1,32,64,128]{3,2,1,0:T(8,128)S(1)}, f32[1,32,64,128]{3,2,1,0:T(8,128)S(1)}, u32[]{:S(2)}, u32[]{:S(2)}) collective-permute-start(f32[1,32,64,128]{3,2,1,0:T(8,128)S(1)} %get-tuple-element.139), channel_id=1, source_target_pairs={{0,16},{1,17},{2,18},{3,19},{4,20},{5,21},{6,22},{7,23},{8,24},{9,... | collective-permute-start | bytes 3145736 | tf_op jit(solution)/shard_map/ppermute | solution.py:14
  96.3 19.2 %collective-permute-done.6 = f32[1,32,64,128]{3,2,1,0:T(8,128)S(1)} collective-permute-done((f32[1,32,64,128]{3,2,1,0:T(8,128)S(1)}, f32[1,32,64,128]{3,2,1,0:T(8,128)S(1)}, u32[]{:S(2)}, u32[]{:S(2)}) %collective-permute-start.6) | collective-permute-done | bytes 1048608 | tf_op jit(solution)/shard_map/ppermute | solution.py:14
  115.5 4.7 %collective-permute-done.7 = f32[1,32,64,128]{3,2,1,0:T(8,128)S(1)} collective-permute-done((f32[1,32,64,128]{3,2,1,0:T(8,128)S(1)}, f32[1,32,64,128]{3,2,1,0:T(8,128)S(1)}, u32[]{:S(2)}, u32[]{:S(2)}) %collective-permute-start.7) | collective-permute-done | bytes 1048608 | tf_op jit(solution)/shard_map/ppermute | solution.py:17
  120.3 4.4 %collective-permute-start.8 = (f32[10,1,64,128]{3,2,1,0:T(8,128)S(1)}, f32[10,1,64,128]{3,2,1,0:T(8,128)S(1)}, u32[]{:S(2)}, u32[]{:S(2)}) collective-permute-start(f32[10,1,64,128]{3,2,1,0:T(8,128)S(1)} %get-tuple-element.131), channel_id=1, source_target_pairs={{0,4},{4,8},{8,12},{1,5},{5,9},{9,13},{2,6},{6,10},{10,14},{3,7},{... | collective-permute-start | bytes 983048 | tf_op jit(solution)/shard_map/ppermute | solution.py:14
  135.9 4.2 %collective-permute-done.11 = f32[10,34,1,128]{3,1,2,0:T(8,128)S(1)} collective-permute-done((f32[10,34,1,128]{3,1,2,0:T(8,128)S(1)}, f32[10,34,1,128]{3,1,2,0:T(8,128)S(1)}, u32[]{:S(2)}, u32[]{:S(2)}) %collective-permute-start.11) | collective-permute-done | bytes 174112 | tf_op jit(solution)/shard_map/ppermute | solution.py:17
  140.3 34.3 %fusion.22 = f32[8,32,64,128]{3,2,1,0:T(8,128)} fusion(f32[8,32,64,128]{3,2,1,0:T(8,128)} %param.7, f32[8,32,64,128]{3,2,1,0:T(8,128)} %copy-done, f32[8,32,64,128]{3,2,1,0:T(8,128)} %param.6, f32[10,34,1,128]{3,2,1,0:T(1,128)S(1)} %copy.31, f32[10,1,64,128]{3,2,1,0:T(8,128)} %copy-done.5, f32[10,1,64,128]{3,2,1,0:T(8,128)S(1)} %collective-permute-done.8, ...), kind=kLoop, calls=%fused_computation.60 | loop fusion | flops 58720256 | bytes 36655104 | tf_op jit(solution)/shard_map/add | solution.py:51
  180.1 19.4 %collective-permute-done.12 = f32[1,32,64,128]{3,2,1,0:T(8,128)S(1)} collective-permute-done((f32[1,32,64,128]{3,2,1,0:T(8,128)S(1)}, f32[1,32,64,128]{3,2,1,0:T(8,128)S(1)}, u32[]{:S(2)}, u32[]{:S(2)}) %collective-permute-start.12) | collective-permute-done | bytes 1048608 | tf_op jit(solution)/shard_map/ppermute | solution.py:14
  199.5 5.0 %collective-permute-done.13 = f32[1,32,64,128]{3,2,1,0:T(8,128)S(1)} collective-permute-done((f32[1,32,64,128]{3,2,1,0:T(8,128)S(1)}, f32[1,32,64,128]{3,2,1,0:T(8,128)S(1)}, u32[]{:S(2)}, u32[]{:S(2)}) %collective-permute-start.13) | collective-permute-done | bytes 1048608 | tf_op jit(solution)/shard_map/ppermute | solution.py:17
  205.6 4.1 %collective-permute-start.14 = (f32[10,1,64,128]{3,2,1,0:T(8,128)S(1)}, f32[10,1,64,128]{3,2,1,0:T(8,128)S(1)}, u32[]{:S(2)}, u32[]{:S(2)}) collective-permute-start(f32[10,1,64,128]{3,2,1,0:T(8,128)S(1)} %get-tuple-element.129), channel_id=1, source_target_pairs={{0,4},{4,8},{8,12},{1,5},{5,9},{9,13},{2,6},{6,10},{10,14},{3,7},{... | collective-permute-start | bytes 983048 | tf_op jit(solution)/shard_map/ppermute | solution.py:14
  220.4 4.2 %collective-permute-done.17 = f32[10,34,1,128]{3,1,2,0:T(8,128)S(1)} collective-permute-done((f32[10,34,1,128]{3,1,2,0:T(8,128)S(1)}, f32[10,34,1,128]{3,1,2,0:T(8,128)S(1)}, u32[]{:S(2)}, u32[]{:S(2)}) %collective-permute-start.17) | collective-permute-done | bytes 174112 | tf_op jit(solution)/shard_map/ppermute | solution.py:17
  224.9 28.6 %fusion.13 = f32[8,32,64,128]{3,2,1,0:T(8,128)} fusion(f32[8,32,64,128]{3,2,1,0:T(8,128)} %param.7, f32[8,32,64,128]{3,2,1,0:T(8,128)} %fusion.22, f32[8,32,64,128]{3,2,1,0:T(8,128)} %param.6, f32[10,34,1,128]{3,2,1,0:T(1,128)S(1)} %copy.35, f32[10,1,64,128]{3,2,1,0:T(8,128)S(1)} %collective-permute-done.15, ...), kind=kLoop, calls=%fused_computation.33 | loop fusion | flops 58720256 | bytes 36655104 | tf_op jit(solution)/shard_map/add | solution.py:51
  258.8 19.4 %collective-permute-done.18 = f32[1,32,64,128]{3,2,1,0:T(8,128)S(1)} collective-permute-done((f32[1,32,64,128]{3,2,1,0:T(8,128)S(1)}, f32[1,32,64,128]{3,2,1,0:T(8,128)S(1)}, u32[]{:S(2)}, u32[]{:S(2)}) %collective-permute-start.18) | collective-permute-done | bytes 1048608 | tf_op jit(solution)/shard_map/ppermute | solution.py:14
  278.2 5.0 %collective-permute-done.19 = f32[1,32,64,128]{3,2,1,0:T(8,128)S(1)} collective-permute-done((f32[1,32,64,128]{3,2,1,0:T(8,128)S(1)}, f32[1,32,64,128]{3,2,1,0:T(8,128)S(1)}, u32[]{:S(2)}, u32[]{:S(2)}) %collective-permute-start.19) | collective-permute-done | bytes 1048608 | tf_op jit(solution)/shard_map/ppermute | solution.py:17
  284.3 3.9 %collective-permute-start.20 = (f32[10,1,64,128]{3,2,1,0:T(8,128)S(1)}, f32[10,1,64,128]{3,2,1,0:T(8,128)S(1)}, u32[]{:S(2)}, u32[]{:S(2)}) collective-permute-start(f32[10,1,64,128]{3,2,1,0:T(8,128)S(1)} %get-tuple-element.127), channel_id=1, source_target_pairs={{0,4},{4,8},{8,12},{1,5},{5,9},{9,13},{2,6},{6,10},{10,14},{3,7},{... | collective-permute-start | bytes 983048 | tf_op jit(solution)/shard_map/ppermute | solution.py:14
  297.5 4.2 %collective-permute-done.23 = f32[10,34,1,128]{3,1,2,0:T(8,128)S(1)} collective-permute-done((f32[10,34,1,128]{3,1,2,0:T(8,128)S(1)}, f32[10,34,1,128]{3,1,2,0:T(8,128)S(1)}, u32[]{:S(2)}, u32[]{:S(2)}) %collective-permute-start.23) | collective-permute-done | bytes 174112 | tf_op jit(solution)/shard_map/ppermute | solution.py:17
  301.9 28.6 %fusion.4 = f32[8,32,64,128]{3,2,1,0:T(8,128)} fusion(f32[8,32,64,128]{3,2,1,0:T(8,128)} %param.7, f32[8,32,64,128]{3,2,1,0:T(8,128)} %fusion.13, f32[8,32,64,128]{3,2,1,0:T(8,128)} %param.6, f32[10,34,1,128]{3,2,1,0:T(1,128)S(1)} %copy.39, f32[10,1,64,128]{3,2,1,0:T(8,128)S(1)} %collective-permute-done.21, ...), kind=kLoop, calls=%fused_computation.6 | loop fusion | flops 58720256 | bytes 36655104 | tf_op jit(solution)/shard_map/add | solution.py:51
  330.5 8.4 %fusion.41 = f32[8,32,64,128]{3,2,1,0:T(8,128)} fusion(f32[8,32,64,128]{3,2,1,0:T(8,128)} %fusion.4), kind=kOutput, calls=%fused_computation.137 | output fusion | flops 65011712 | bytes 16777216 | tf_op jit(solution)/shard_map/jit(cumsum)/reduce_window_sum | solution.py:58
  340.6 17.2 %all-gather.3.cloned.1.call-done = f32[32,1,64,128]{3,2,1,0:T(8,128)} async-done(((f32[8,1,64,128]{3,2,1,0:T(8,128)}), f32[32,1,64,128]{3,2,1,0:T(8,128)}) %all-gather.3.cloned.1.call-update) | async-done | bytes 1048592 | tf_op jit(solution)/shard_map/all_gather | solution.py:24
  361.0 8.8 %add_multiply_fusion = f32[8,32,64,128]{3,2,1,0:T(8,128)} fusion(f32[8,32,64,128]{3,2,1,0:T(8,128)} %fusion.41, f32[8,64,128]{2,1,0:T(8,128)S(1)} %bitcast.13), kind=kLoop, calls=%fused_computation.101 | loop fusion | flops 4194304 | bytes 17039360 | tf_op jit(solution)/shard_map/div | solution.py:67
  (92 shorter events, 71.9 us)
Async XLA Ops:
  7.2 350.7 %all-gather.3.cloned.1.call-start = ((), (), s32[]{:S(2)}) async-start(), calls=%async_computation | async-start | bytes 1310720 | tf_op jit(solution)/shard_map/all_gather | solution.py:24
  8.9 27.3 %collective-permute-start = (f32[1,32,64,128]{3,2,1,0:T(8,128)S(1)}, f32[1,32,64,128]{3,2,1,0:T(8,128)S(1)}, u32[]{:S(2)}, u32[]{:S(2)}) collective-permute-start(f32[1,32,64,128]{3,2,1,0:T(8,128)S(1)} %get-tuple-element.142), channel_id=1, source_target_pairs={{0,16},{1,17},{2,18},{3,19},{4,20},{5,21},{6,22},{7,23},{8,24},{9,... | collective-permute-start | bytes 3145736 | tf_op jit(solution)/shard_map/ppermute | solution.py:14
  13.8 26.6 %collective-permute-start.1 = (f32[1,32,64,128]{3,2,1,0:T(8,128)S(1)}, f32[1,32,64,128]{3,2,1,0:T(8,128)S(1)}, u32[]{:S(2)}, u32[]{:S(2)}) collective-permute-start(f32[1,32,64,128]{3,2,1,0:T(8,128)S(1)} %get-tuple-element.141), channel_id=1, source_target_pairs={{16,0},{17,1},{18,2},{19,3},{20,4},{21,5},{22,6},{23,7},{24,8},{25... | collective-permute-start | bytes 3145736 | tf_op jit(solution)/shard_map/ppermute | solution.py:17
  42.0 5.3 %collective-permute-start.3 = (f32[10,1,64,128]{3,2,1,0:T(8,128)S(1)}, f32[10,1,64,128]{3,2,1,0:T(8,128)S(1)}, u32[]{:S(2)}, u32[]{:S(2)}) collective-permute-start(f32[10,1,64,128]{3,2,1,0:T(8,128)S(1)} %get-tuple-element.134), channel_id=1, source_target_pairs={{4,0},{8,4},{12,8},{5,1},{9,5},{13,9},{6,2},{10,6},{14,10},{7,3},{... | collective-permute-start | bytes 983048 | tf_op jit(solution)/shard_map/ppermute | solution.py:17
  47.5 6.7 %collective-permute-start.4 = (f32[10,34,1,128]{3,1,2,0:T(8,128)S(1)}, f32[10,34,1,128]{3,1,2,0:T(8,128)S(1)}, u32[]{:S(2)}, u32[]{:S(2)}) collective-permute-start(f32[10,34,1,128]{3,1,2,0:T(8,128)S(1)} %copy.24), channel_id=1, source_target_pairs={{0,1},{1,2},{2,3},{4,5},{5,6},{6,7},{8,9},{9,10},{10,11},{12,13},{... | collective-permute-start | bytes 522248 | tf_op jit(solution)/shard_map/ppermute | solution.py:14
  51.1 7.7 %collective-permute-start.5 = (f32[10,34,1,128]{3,1,2,0:T(8,128)S(1)}, f32[10,34,1,128]{3,1,2,0:T(8,128)S(1)}, u32[]{:S(2)}, u32[]{:S(2)}) collective-permute-start(f32[10,34,1,128]{3,1,2,0:T(8,128)S(1)} %copy.26), channel_id=1, source_target_pairs={{1,0},{2,1},{3,2},{5,4},{6,5},{7,6},{9,8},{10,9},{11,10},{13,12},{... | collective-permute-start | bytes 522248 | tf_op jit(solution)/shard_map/ppermute | solution.py:17
  90.5 25.0 %collective-permute-start.6 = (f32[1,32,64,128]{3,2,1,0:T(8,128)S(1)}, f32[1,32,64,128]{3,2,1,0:T(8,128)S(1)}, u32[]{:S(2)}, u32[]{:S(2)}) collective-permute-start(f32[1,32,64,128]{3,2,1,0:T(8,128)S(1)} %get-tuple-element.139), channel_id=1, source_target_pairs={{0,16},{1,17},{2,18},{3,19},{4,20},{5,21},{6,22},{7,23},{8,24},{9,... | collective-permute-start | bytes 3145736 | tf_op jit(solution)/shard_map/ppermute | solution.py:14
  95.0 25.2 %collective-permute-start.7 = (f32[1,32,64,128]{3,2,1,0:T(8,128)S(1)}, f32[1,32,64,128]{3,2,1,0:T(8,128)S(1)}, u32[]{:S(2)}, u32[]{:S(2)}) collective-permute-start(f32[1,32,64,128]{3,2,1,0:T(8,128)S(1)} %get-tuple-element.140), channel_id=1, source_target_pairs={{16,0},{17,1},{18,2},{19,3},{20,4},{21,5},{22,6},{23,7},{24,8},{25... | collective-permute-start | bytes 3145736 | tf_op jit(solution)/shard_map/ppermute | solution.py:17
  120.3 5.7 %collective-permute-start.8 = (f32[10,1,64,128]{3,2,1,0:T(8,128)S(1)}, f32[10,1,64,128]{3,2,1,0:T(8,128)S(1)}, u32[]{:S(2)}, u32[]{:S(2)}) collective-permute-start(f32[10,1,64,128]{3,2,1,0:T(8,128)S(1)} %get-tuple-element.131), channel_id=1, source_target_pairs={{0,4},{4,8},{8,12},{1,5},{5,9},{9,13},{2,6},{6,10},{10,14},{3,7},{... | collective-permute-start | bytes 983048 | tf_op jit(solution)/shard_map/ppermute | solution.py:14
  124.7 3.5 collective-permute-start.9
  129.0 6.7 %collective-permute-start.10 = (f32[10,34,1,128]{3,1,2,0:T(8,128)S(1)}, f32[10,34,1,128]{3,1,2,0:T(8,128)S(1)}, u32[]{:S(2)}, u32[]{:S(2)}) collective-permute-start(f32[10,34,1,128]{3,1,2,0:T(8,128)S(1)} %copy.28), channel_id=1, source_target_pairs={{0,1},{1,2},{2,3},{4,5},{5,6},{6,7},{8,9},{9,10},{10,11},{12,13},{... | collective-permute-start | bytes 522248 | tf_op jit(solution)/shard_map/ppermute | solution.py:14
  132.5 7.7 %collective-permute-start.11 = (f32[10,34,1,128]{3,1,2,0:T(8,128)S(1)}, f32[10,34,1,128]{3,1,2,0:T(8,128)S(1)}, u32[]{:S(2)}, u32[]{:S(2)}) collective-permute-start(f32[10,34,1,128]{3,1,2,0:T(8,128)S(1)} %copy.30), channel_id=1, source_target_pairs={{1,0},{2,1},{3,2},{5,4},{6,5},{7,6},{9,8},{10,9},{11,10},{13,12},{... | collective-permute-start | bytes 522248 | tf_op jit(solution)/shard_map/ppermute | solution.py:17
  176.5 22.9 %collective-permute-start.12 = (f32[1,32,64,128]{3,2,1,0:T(8,128)S(1)}, f32[1,32,64,128]{3,2,1,0:T(8,128)S(1)}, u32[]{:S(2)}, u32[]{:S(2)}) collective-permute-start(f32[1,32,64,128]{3,2,1,0:T(8,128)S(1)} %get-tuple-element.137), channel_id=1, source_target_pairs={{0,16},{1,17},{2,18},{3,19},{4,20},{5,21},{6,22},{7,23},{8,24},{9,... | collective-permute-start | bytes 3145736 | tf_op jit(solution)/shard_map/ppermute | solution.py:14
  178.5 26.0 %collective-permute-start.13 = (f32[1,32,64,128]{3,2,1,0:T(8,128)S(1)}, f32[1,32,64,128]{3,2,1,0:T(8,128)S(1)}, u32[]{:S(2)}, u32[]{:S(2)}) collective-permute-start(f32[1,32,64,128]{3,2,1,0:T(8,128)S(1)} %get-tuple-element.138), channel_id=1, source_target_pairs={{16,0},{17,1},{18,2},{19,3},{20,4},{21,5},{22,6},{23,7},{24,8},{25... | collective-permute-start | bytes 3145736 | tf_op jit(solution)/shard_map/ppermute | solution.py:17
  205.6 5.4 %collective-permute-start.14 = (f32[10,1,64,128]{3,2,1,0:T(8,128)S(1)}, f32[10,1,64,128]{3,2,1,0:T(8,128)S(1)}, u32[]{:S(2)}, u32[]{:S(2)}) collective-permute-start(f32[10,1,64,128]{3,2,1,0:T(8,128)S(1)} %get-tuple-element.129), channel_id=1, source_target_pairs={{0,4},{4,8},{8,12},{1,5},{5,9},{9,13},{2,6},{6,10},{10,14},{3,7},{... | collective-permute-start | bytes 983048 | tf_op jit(solution)/shard_map/ppermute | solution.py:14
  209.7 3.5 collective-permute-start.15
  213.5 6.7 %collective-permute-start.16 = (f32[10,34,1,128]{3,1,2,0:T(8,128)S(1)}, f32[10,34,1,128]{3,1,2,0:T(8,128)S(1)}, u32[]{:S(2)}, u32[]{:S(2)}) collective-permute-start(f32[10,34,1,128]{3,1,2,0:T(8,128)S(1)} %copy.32), channel_id=1, source_target_pairs={{0,1},{1,2},{2,3},{4,5},{5,6},{6,7},{8,9},{9,10},{10,11},{12,13},{... | collective-permute-start | bytes 522248 | tf_op jit(solution)/shard_map/ppermute | solution.py:14
  217.0 7.7 %collective-permute-start.17 = (f32[10,34,1,128]{3,1,2,0:T(8,128)S(1)}, f32[10,34,1,128]{3,1,2,0:T(8,128)S(1)}, u32[]{:S(2)}, u32[]{:S(2)}) collective-permute-start(f32[10,34,1,128]{3,1,2,0:T(8,128)S(1)} %copy.34), channel_id=1, source_target_pairs={{1,0},{2,1},{3,2},{5,4},{6,5},{7,6},{9,8},{10,9},{11,10},{13,12},{... | collective-permute-start | bytes 522248 | tf_op jit(solution)/shard_map/ppermute | solution.py:17
  255.3 22.9 %collective-permute-start.18 = (f32[1,32,64,128]{3,2,1,0:T(8,128)S(1)}, f32[1,32,64,128]{3,2,1,0:T(8,128)S(1)}, u32[]{:S(2)}, u32[]{:S(2)}) collective-permute-start(f32[1,32,64,128]{3,2,1,0:T(8,128)S(1)} %get-tuple-element.135), channel_id=1, source_target_pairs={{0,16},{1,17},{2,18},{3,19},{4,20},{5,21},{6,22},{7,23},{8,24},{9,... | collective-permute-start | bytes 3145736 | tf_op jit(solution)/shard_map/ppermute | solution.py:14
  257.3 26.0 %collective-permute-start.19 = (f32[1,32,64,128]{3,2,1,0:T(8,128)S(1)}, f32[1,32,64,128]{3,2,1,0:T(8,128)S(1)}, u32[]{:S(2)}, u32[]{:S(2)}) collective-permute-start(f32[1,32,64,128]{3,2,1,0:T(8,128)S(1)} %get-tuple-element.136), channel_id=1, source_target_pairs={{16,0},{17,1},{18,2},{19,3},{20,4},{21,5},{22,6},{23,7},{24,8},{25... | collective-permute-start | bytes 3145736 | tf_op jit(solution)/shard_map/ppermute | solution.py:17
  284.3 5.2 %collective-permute-start.20 = (f32[10,1,64,128]{3,2,1,0:T(8,128)S(1)}, f32[10,1,64,128]{3,2,1,0:T(8,128)S(1)}, u32[]{:S(2)}, u32[]{:S(2)}) collective-permute-start(f32[10,1,64,128]{3,2,1,0:T(8,128)S(1)} %get-tuple-element.127), channel_id=1, source_target_pairs={{0,4},{4,8},{8,12},{1,5},{5,9},{9,13},{2,6},{6,10},{10,14},{3,7},{... | collective-permute-start | bytes 983048 | tf_op jit(solution)/shard_map/ppermute | solution.py:14
  288.3 3.5 collective-permute-start.21
  292.1 5.2 %collective-permute-start.22 = (f32[10,34,1,128]{3,1,2,0:T(8,128)S(1)}, f32[10,34,1,128]{3,1,2,0:T(8,128)S(1)}, u32[]{:S(2)}, u32[]{:S(2)}) collective-permute-start(f32[10,34,1,128]{3,1,2,0:T(8,128)S(1)} %copy.36), channel_id=1, source_target_pairs={{0,1},{1,2},{2,3},{4,5},{5,6},{6,7},{8,9},{9,10},{10,11},{12,13},{... | collective-permute-start | bytes 522248 | tf_op jit(solution)/shard_map/ppermute | solution.py:14
  294.1 7.7 %collective-permute-start.23 = (f32[10,34,1,128]{3,1,2,0:T(8,128)S(1)}, f32[10,34,1,128]{3,1,2,0:T(8,128)S(1)}, u32[]{:S(2)}, u32[]{:S(2)}) collective-permute-start(f32[10,34,1,128]{3,1,2,0:T(8,128)S(1)} %copy.38), channel_id=1, source_target_pairs={{1,0},{2,1},{3,2},{5,4},{6,5},{7,6},{9,8},{10,9},{11,10},{13,12},{... | collective-permute-start | bytes 522248 | tf_op jit(solution)/shard_map/ppermute | solution.py:17
  (11 other events, 243.7 us)
Sparse Core Ops, SparseCore 0:
  340.8 17.0 all-gather.2
where the time goes:
time: 378 us; the launch traced here: 377 us
  waiting for transfers between devices  146 us (39%)
  other arithmetic  146 us (39%)
  starting transfers between devices  55.5 us (15%)
  local copies, waits for them, and re-layouts  15 us (4%)
  between operations  14.5 us (4%)
    add x4, other arithmetic, explicit_update(): return middle + scaled_diffusivity * spread + scaled_forcing  122 us
    ppermute x12, waiting for transfers between devices, extended(): lax.ppermute(lax.slice_in_dim(block, block.shape[dim] - width, None, axis...  86.8 us
    ppermute x12, waiting for transfers between devices, extended(): lax.ppermute(lax.slice_in_dim(block, 0, width, axis=dim), axis, backward)  41.7 us
    ppermute x12, starting transfers between devices, extended(): lax.ppermute(lax.slice_in_dim(block, block.shape[dim] - width, None, axis...  39.5 us
    all_gather x1, waiting for transfers between devices, prefix(): pieces = lax.all_gather(value, axis)  17.2 us
    ppermute x12, starting transfers between devices, extended(): lax.ppermute(lax.slice_in_dim(block, 0, width, axis=dim), axis, backward)  16 us
    div x1, other arithmetic, per_device(): (present_layer + previous_plane) / (initial_state.shape[1] * lax.axis_siz...  8.81 us
    another operation x1, other arithmetic, per_device(): present_layer = jnp.cumsum(initial_state, axis=1)  8.42 us
  transfers between devices with their start and end apart: 25, of which 20 were waited for; matrix products, arithmetic and copies ran while one was open for 2% of the time, Pallas kernels for 0%

commit v1 on v0

v1 whole, which is shorter than its diff:
```python
import functools

import jax
import jax.numpy as jnp
from jax import lax
from jax.experimental import pallas as pl
from jax.experimental.pallas import tpu as pltpu
from jax.sharding import PartitionSpec as P

STEPS = 4
PAD = 8
CHUNK = 8
MESH = pl.DeviceIdType.MESH


def steps_kernel(
    sizes, x, d, f, end, before, state, coef, source,
    lev_out, lev_in, tot_mid, tot_edge, mid_in, edge_in,
    lat_send, lat_recv, lon_send, lon_recv, lev_send, lev_recv,
    load_sem, end_sem, tot_send, tot_recv,
):
    J, I, K, M = x.shape
    chunks = K // CHUNK
    me = {axis: lax.axis_index(axis) for axis in sizes}
    n_lon = sizes["lon"]
    rows = pl.ds(1, I)
    levels = pl.ds(PAD, K)
    planes = pl.ds(1, J)

    def has(axis, side):
        return me[axis] > 0 if side == 0 else me[axis] < sizes[axis] - 1

    def beside(axis, side):
        return {axis: me[axis] - 1 if side == 0 else me[axis] + 1}

    def both(axis, act):
        if sizes[axis] > 1:
            for side in (0, 1):
                pl.when(has(axis, side))(functools.partial(act, side))

    def load(which, j):
        src, dst = (
            (x.at[j], state.at[0, j + 1, rows, levels]),
            (d.at[j], coef.at[j]),
            (f.at[j], source.at[j]),
        )[which]
        return pltpu.make_async_copy(src, dst, load_sem.at[which, j])

    for which in range(3):
        for j in range(J):
            load(which, j).start()

    barrier = pltpu.get_barrier_semaphore()
    count = jnp.int32(n_lon - 1)

    def greet(target):
        pl.semaphore_signal(barrier, inc=1, device_id=target, device_id_type=MESH)

    for axis in ("lat", "lev"):
        both(axis, lambda side, axis=axis: greet(beside(axis, side)))
        if sizes[axis] > 1:
            count = count + has(axis, 0).astype(jnp.int32) + has(axis, 1).astype(jnp.int32)
    for other in range(n_lon):
        pl.when(other != me["lon"])(lambda other=other: greet({"lon": jnp.int32(other)}))
    pl.semaphore_wait(barrier, count)

    def lat_copy(step, side, c):
        slot = step % 2
        part = pl.ds(pl.multiple_of(PAD + c * CHUNK, CHUNK), CHUNK)
        plane, target = (1, J + 1) if side == 0 else (J, 0)
        if step == 0:
            inner = pl.ds(pl.multiple_of(c * CHUNK, CHUNK), CHUNK)
            src = x.at[plane - 1, :, inner]
        else:
            src = state.at[slot, plane, rows, part]
        return pltpu.make_async_remote_copy(
            src_ref=src,
            dst_ref=state.at[slot, target, rows, part],
            send_sem=lat_send.at[slot, side, c],
            recv_sem=lat_recv.at[slot, 1 - side, c],
            device_id=beside("lat", side),
            device_id_type=MESH,
        )

    def lat_arrived(step, side, c):
        slot = step % 2
        part = pl.ds(pl.multiple_of(PAD + c * CHUNK, CHUNK), CHUNK)
        target = 0 if side == 0 else J + 1
        pltpu.make_async_remote_copy(
            src_ref=state.at[slot, target, rows, part],
            dst_ref=state.at[slot, target, rows, part],
            send_sem=lat_send.at[slot, side, c],
            recv_sem=lat_recv.at[slot, side, c],
            device_id=beside("lat", side),
            device_id_type=MESH,
        ).wait_recv()

    def lon_copy(step, side, arriving=False):
        slot = step % 2
        row, target = (1, I + 1) if side == 0 else (I, 0)
        dst = (0 if side == 0 else I + 1) if arriving else target
        return pltpu.make_async_remote_copy(
            src_ref=state.at[slot, planes, row, levels],
            dst_ref=state.at[slot, planes, dst, levels],
            send_sem=lon_send.at[slot, side],
            recv_sem=lon_recv.at[slot, side if arriving else 1 - side],
            device_id=beside("lon", side),
            device_id_type=MESH,
        )

    def lev_copy(step, side, arriving=False):
        slot = step % 2
        landing = side if arriving else 1 - side
        return pltpu.make_async_remote_copy(
            src_ref=lev_out.at[side],
            dst_ref=lev_in.at[slot, landing],
            send_sem=lev_send.at[slot, side],
            recv_sem=lev_recv.at[slot, landing],
            device_id=beside("lev", side),
            device_id_type=MESH,
        )

    def lat_start(step, c):
        both("lat", lambda side: lat_copy(step, side, c).start())

    for c in range(chunks):
        lat_start(0, c)

    def clear(axis, side):
        for slot in (0, 1):
            if axis == "lat":
                target = 0 if side == 0 else J + 1

                @pl.loop(1, I + 1)
                def _(i):
                    state[slot, target, i, PAD : PAD + K, :] = jnp.zeros((K, M), jnp.float32)
            elif axis == "lon":
                target = 0 if side == 0 else I + 1
                for p in range(1, J + 1):
                    state[slot, p, target, PAD : PAD + K, :] = jnp.zeros((K, M), jnp.float32)
            else:
                target = PAD - 1 if side == 0 else PAD + K

                @pl.loop(1, J + 1)
                def _(p):
                    state[slot, p, 1 : I + 1, target : target + 1, :] = jnp.zeros(
                        (I, 1, M), jnp.float32
                    )

    for axis in ("lat", "lon", "lev"):
        for side in (0, 1):
            pl.when(jnp.logical_not(has(axis, side)))(functools.partial(clear, axis, side))

    for j in range(J):
        load(0, j).wait()

    def update(step, p, i, start, length):
        a, b = step % 2, (step + 1) % 2
        here = pl.ds(start, length)
        inner = pl.ds(start - PAD, length)
        middle = state[a, p, i, here, :]
        spread = (
            (state[a, p - 1, i, here, :] + state[a, p + 1, i, here, :])
            + (state[a, p, i - 1, here, :] + state[a, p, i + 1, here, :])
            + (
                state[a, p, i, pl.ds(start - 1, length), :]
                + state[a, p, i, pl.ds(start + 1, length), :]
            )
            - 6.0 * middle
        )
        new = middle + coef[p - 1, i - 1, inner, :] * spread + source[p - 1, i - 1, inner, :]
        state[b, p, i, here, :] = new
        return new

    def mid_total(target, arriving=None):
        sender = me["lon"] if arriving is None else arriving
        return pltpu.make_async_remote_copy(
            src_ref=tot_mid,
            dst_ref=mid_in.at[sender],
            send_sem=tot_send.at[target, chunks],
            recv_sem=tot_recv.at[sender, chunks],
            device_id={"lon": jnp.int32(target)},
            device_id_type=MESH,
        )

    def edge_total(target, c, arriving=None):
        sender = me["lon"] if arriving is None else arriving
        part = pl.ds(pl.multiple_of(c * CHUNK, CHUNK), CHUNK)
        return pltpu.make_async_remote_copy(
            src_ref=tot_edge.at[:, part],
            dst_ref=edge_in.at[sender, :, part],
            send_sem=tot_send.at[target, c],
            recv_sem=tot_recv.at[sender, c],
            device_id={"lon": jnp.int32(target)},
            device_id_type=MESH,
        )

    def later(act):
        for other in range(1, n_lon):
            pl.when(other > me["lon"])(functools.partial(act, other))

    def earlier(act):
        for other in range(n_lon - 1):
            pl.when(other < me["lon"])(functools.partial(act, other))

    final = STEPS % 2

    def mid_end():
        return pltpu.make_async_copy(
            state.at[final, pl.ds(2, J - 2), rows, levels],
            end.at[pl.ds(1, J - 2)],
            end_sem.at[2, 0],
        )

    def edge_end(which, c):
        plane = 1 if which == 0 else J
        part = pl.ds(pl.multiple_of(PAD + c * CHUNK, CHUNK), CHUNK)
        inner = pl.ds(pl.multiple_of(c * CHUNK, CHUNK), CHUNK)
        return pltpu.make_async_copy(
            state.at[final, plane, rows, part],
            end.at[plane - 1, :, inner],
            end_sem.at[which, c],
        )

    for step in range(STEPS):
        a, b = step % 2, (step + 1) % 2
        last = step == STEPS - 1

        both("lon", lambda side: lon_copy(step, side).start())
        if sizes["lev"] > 1:

            @pl.loop(1, J + 1)
            def _(p):
                lev_out[0, p - 1] = state[a, p, 1 : I + 1, PAD : PAD + 1, :]
                lev_out[1, p - 1] = state[a, p, 1 : I + 1, PAD + K - 1 : PAD + K, :]

        both("lev", lambda side: lev_copy(step, side).start())
        if step == 0:
            for j in range(J):
                load(1, j).wait()
                load(2, j).wait()

        def lon_done(side):
            lon_copy(step, side).wait_send()
            lon_copy(step, side, True).wait_recv()

        def lev_done(side):
            lev_copy(step, side).wait_send()
            lev_copy(step, side, True).wait_recv()
            row = PAD - 1 if side == 0 else PAD + K

            @pl.loop(1, J + 1)
            def _(p):
                state[a, p, 1 : I + 1, row : row + 1, :] = lev_in[a, side, p - 1]

        both("lon", lon_done)
        both("lev", lev_done)

        @pl.loop(2, J)
        def _(p):
            if last:
                tot_mid[p - 2] = lax.fori_loop(
                    1,
                    I + 1,
                    lambda i, total: total + update(step, p, i, PAD, K),
                    jnp.zeros((K, M), jnp.float32),
                )
            else:

                @pl.loop(1, I + 1)
                def _(i):
                    update(step, p, i, PAD, K)

        if last:
            mid_end().start()
            later(lambda other: mid_total(other).start())

        @pl.loop(0, chunks)
        def _(c):
            def ready(side):
                if step > 0:
                    lat_copy(step - 1, side, c).wait_send()
                lat_arrived(step, side, c)

            both("lat", ready)
            start = pl.multiple_of(PAD + c * CHUNK, CHUNK)
            zero = jnp.zeros((CHUNK, M), jnp.float32)

            def row(i, totals):
                return (
                    totals[0] + update(step, 1, i, start, CHUNK),
                    totals[1] + update(step, J, i, start, CHUNK),
                )

            low, high = lax.fori_loop(1, I + 1, row, (zero, zero), unroll=4)
            if last:
                part = pl.ds(pl.multiple_of(c * CHUNK, CHUNK), CHUNK)
                tot_edge[0, part, :] = low
                tot_edge[1, part, :] = high
                later(lambda other: edge_total(other, c).start())
                edge_end(0, c).start()
                edge_end(1, c).start()
            else:
                lat_start(step + 1, c)

    before[...] = jnp.zeros(before.shape, jnp.float32)

    def add_mid(other):
        mid_total(other, other).wait_recv()
        before[1 : J - 1] += mid_in[other]

    def add_edge(other):
        for c in range(chunks):
            edge_total(other, c, other).wait_recv()
        before[0] += edge_in[other, 0]
        before[J - 1] += edge_in[other, 1]

    earlier(add_mid)
    earlier(add_edge)

    for c in range(chunks):
        both("lat", lambda side: lat_copy(STEPS - 1, side, c).wait_send())
        later(lambda other: edge_total(other, c).wait_send())
        edge_end(0, c).wait()
        edge_end(1, c).wait()
    later(lambda other: mid_total(other).wait_send())
    mid_end().wait()


def totals_kernel(scale, x, before, totals, end):
    def row(i, total):
        value = x[0, i]
        total = total + value
        totals[0, i] = total * scale
        end[0, i] = value
        return total

    lax.fori_loop(0, x.shape[1], row, before[0], unroll=4)


def per_device(sizes, initial_state, scaled_diffusivity, scaled_forcing):
    J, I, K, M = initial_state.shape
    chunks = K // CHUNK
    n_lon = sizes["lon"]
    f32 = jnp.float32
    vmem = lambda *shape: pltpu.VMEM(shape, f32)
    sem = lambda *shape: pltpu.SemaphoreType.DMA(shape)
    hbm = pl.BlockSpec(memory_space=pltpu.HBM)
    end, before = pl.pallas_call(
        functools.partial(steps_kernel, sizes),
        out_shape=(
            jax.ShapeDtypeStruct((J, I, K, M), f32),
            jax.ShapeDtypeStruct((J, K, M), f32),
        ),
        in_specs=[hbm] * 3,
        out_specs=(hbm, pl.BlockSpec(memory_space=pltpu.VMEM)),
        scratch_shapes=[
            vmem(2, J + 2, I + 2, K + 2 * PAD, M),
            vmem(J, I, K, M),
            vmem(J, I, K, M),
            vmem(2, J, I, 1, M),
            vmem(2, 2, J, I, 1, M),
            vmem(J - 2, K, M),
            vmem(2, K, M),
            vmem(n_lon, J - 2, K, M),
            vmem(n_lon, 2, K, M),
            sem(2, 2, chunks),
            sem(2, 2, chunks),
            sem(2, 2),
            sem(2, 2),
            sem(2, 2),
            sem(2, 2),
            sem(3, J),
            sem(3, chunks),
            sem(n_lon, chunks + 1),
            sem(n_lon, chunks + 1),
        ],
        compiler_params=pltpu.CompilerParams(
            collective_id=0, has_side_effects=True, vmem_limit_bytes=58 * 2**20
        ),
        name="steps",
    )(initial_state, scaled_diffusivity, scaled_forcing)

    half = K // 2
    block = pl.BlockSpec((1, I, half, M), lambda j, k: (j, 0, k, 0))
    return pl.pallas_call(
        functools.partial(totals_kernel, 1.0 / (I * n_lon)),
        grid=(J, K // half),
        out_shape=(jax.ShapeDtypeStruct((J, I, K, M), f32),) * 2,
        in_specs=[block, pl.BlockSpec((1, half, M), lambda j, k: (j, k, 0))],
        out_specs=(block, block),
        name="totals",
    )(end, before)


def solution(mesh):
    spec = P("lat", "lon", "lev", None)
    return jax.shard_map(
        functools.partial(per_device, dict(mesh.shape)),
        mesh=mesh,
        in_specs=(spec,) * 3,
        out_specs=(spec,) * 2,
        check_vma=False,
    )
```

time: 378 us -> 115 us (0.30)
  other arithmetic: 146 us -> 0 us
  waiting for transfers between devices: 146 us -> 0 us
  Pallas kernels: 0 us -> 114 us
  starting transfers between devices: 55.5 us -> 0 us
  local copies, waits for them, and re-layouts: 15 us -> 0 us
  between operations: 14.5 us -> 0.64 us
    ppermute x24 -> x0, waiting for transfers between devices: 128 us -> none  [the longest x12 86.8 us: extended(): lax.ppermute(lax.slice_in_dim(block, block.shape[dim] - width, None, axis...]
    add x4 -> x0, other arithmetic: 122 us -> none  [explicit_update(): return middle + scaled_diffusivity * spread + scaled_forcing]
    pallas_call x0 -> x2, Pallas kernels: none -> 114 us  [the longest x1 100 us: per_device(): pl.pallas_call(functools.partial(steps_kernel, sizes), out_shape=(jax.Sha...]
    ppermute x24 -> x0, starting transfers between devices: 55.5 us -> none  [the longest x12 39.5 us: extended(): lax.ppermute(lax.slice_in_dim(block, block.shape[dim] - width, None, axis...]
    all_gather x1 -> x0, waiting for transfers between devices: 17.2 us -> none  [prefix(): pieces = lax.all_gather(value, axis)]
    div x1 -> x0, other arithmetic: 8.81 us -> none  [per_device(): (present_layer + previous_plane) / (initial_state.shape[1] * lax.axis_siz...]
    another operation x1 -> x0, other arithmetic: 8.42 us -> none  [per_device(): present_layer = jnp.cumsum(initial_state, axis=1)]
    slice x14 -> x0, local copies, waits for them, and re-layouts: 7.32 us -> none  [the longest x8 3.91 us: extended(): lax.slice_in_dim(block, block.shape[dim] - width, None, axis=dim)]
  transfers between devices with their start and end apart: 25 -> 0, of which waited for: 20 -> 0; matrix products, arithmetic and copies ran while one was open for 2% -> 0% of each run, Pallas kernels for 0% -> 0%
where the time goes in v1:
time: 115 us
  Pallas kernels  114 us (99%)
    pallas_call x1, Pallas kernels, per_device(): pl.pallas_call(functools.partial(steps_kernel, sizes), out_shape=(jax.Sha...  100 us
    pallas_call x1, Pallas kernels, per_device(): pl.pallas_call(functools.partial(totals_kernel, 1.0 / (I * n_lon)), grid=...  13.7 us

profile of v1, /device:TPU:0, one launch (start us, length us, event | category | flops | bytes accessed | tf_op | source)
XLA Modules:
  0.0 114.5 jit_solution(3391446300430280981)
XLA Ops:
  0.6 100.2 %steps.1 = (f32[8,32,64,128]{3,2,1,0:T(8,128)}, f32[8,64,128]{2,1,0:T(8,128)}) custom-call(f32[8,32,64,128]{3,2,1,0:T(8,128)} %x.1, f32[8,32,64,128]{3,2,1,0:T(8,128)} %d.1, f32[8,32,64,128]{3,2,1,0:T(8,128)} %f.1), custom_call_target="tpu_custom_call" | custom-call | tf_op jit(solution)/shard_map/steps/pallas_call | solution.py:349
  100.9 13.7 %totals.1 = (f32[8,32,64,128]{3,2,1,0:T(8,128)}, f32[8,32,64,128]{3,2,1,0:T(8,128)}) custom-call(f32[8,32,64,128]{3,2,1,0:T(8,128)} %get-tuple-element.4.x, f32[8,64,128]{2,1,0:T(8,128)} %get-tuple-element.5.before), custom_call_target="tpu_custom_call" | custom-call | tf_op jit(solution)/shard_map/totals/pallas_call | solution.py:386

commit v2 on v1

--- a/solution.py
+++ b/solution.py
@@ -17,7 +17,7 @@
     sizes, x, d, f, end, before, state, coef, source,
     lev_out, lev_in, tot_mid, tot_edge, mid_in, edge_in,
     lat_send, lat_recv, lon_send, lon_recv, lev_send, lev_recv,
-    load_sem, end_sem, tot_send, tot_recv,
+    load_sem, tot_send, tot_recv,
 ):
     J, I, K, M = x.shape
     chunks = K // CHUNK
@@ -45,10 +45,6 @@
             (f.at[j], source.at[j]),
         )[which]
         return pltpu.make_async_copy(src, dst, load_sem.at[which, j])
-
-    for which in range(3):
-        for j in range(J):
-            load(which, j).start()
 
     barrier = pltpu.get_barrier_semaphore()
     count = jnp.int32(n_lon - 1)
@@ -126,6 +122,10 @@
     for c in range(chunks):
         lat_start(0, c)
 
+    for which in range(3):
+        for j in range(J):
+            load(which, j).start()
+
     def clear(axis, side):
         for slot in (0, 1):
             if axis == "lat":
@@ -169,7 +169,10 @@
             - 6.0 * middle
         )
         new = middle + coef[p - 1, i - 1, inner, :] * spread + source[p - 1, i - 1, inner, :]
-        state[b, p, i, here, :] = new
+        if step == STEPS - 1:
+            end[p - 1, i - 1, inner, :] = new
+        else:
+            state[b, p, i, here, :] = new
         return new
 
     def mid_total(target, arriving=None):
@@ -203,24 +206,26 @@
         for other in range(n_lon - 1):
             pl.when(other < me["lon"])(functools.partial(act, other))
 
-    final = STEPS % 2
-
-    def mid_end():
-        return pltpu.make_async_copy(
-            state.at[final, pl.ds(2, J - 2), rows, levels],
-            end.at[pl.ds(1, J - 2)],
-            end_sem.at[2, 0],
-        )
-
-    def edge_end(which, c):
-        plane = 1 if which == 0 else J
-        part = pl.ds(pl.multiple_of(PAD + c * CHUNK, CHUNK), CHUNK)
-        inner = pl.ds(pl.multiple_of(c * CHUNK, CHUNK), CHUNK)
-        return pltpu.make_async_copy(
-            state.at[final, plane, rows, part],
-            end.at[plane - 1, :, inner],
-            end_sem.at[which, c],
-        )
+    def add_mids():
+        before[...] = jnp.zeros(before.shape, jnp.float32)
+
+        def add(other):
+            mid_total(other, other).wait_recv()
+            before[1 : J - 1] += mid_in[other]
+
+        earlier(add)
+        for c in range(chunks // 2):
+            add_edges(c)
+
+    def add_edges(c):
+        part = pl.ds(pl.multiple_of(c * CHUNK, CHUNK), CHUNK)
+
+        def add(other):
+            edge_total(other, c, other).wait_recv()
+            before[0, part, :] += edge_in[other, 0, part, :]
+            before[J - 1, part, :] += edge_in[other, 1, part, :]
+
+        earlier(add)
 
     for step in range(STEPS):
         a, b = step % 2, (step + 1) % 2
@@ -272,7 +277,6 @@
                     update(step, p, i, PAD, K)
 
         if last:
-            mid_end().start()
             later(lambda other: mid_total(other).start())
 
         @pl.loop(0, chunks)
@@ -298,44 +302,45 @@
                 tot_edge[0, part, :] = low
                 tot_edge[1, part, :] = high
                 later(lambda other: edge_total(other, c).start())
-                edge_end(0, c).start()
-                edge_end(1, c).start()
+                pl.when(c == chunks // 2)(add_mids)
+
+                @pl.when(c > chunks // 2)
+                def _():
+                    add_edges(c - 1)
             else:
                 lat_start(step + 1, c)
 
-    before[...] = jnp.zeros(before.shape, jnp.float32)
-
-    def add_mid(other):
-        mid_total(other, other).wait_recv()
-        before[1 : J - 1] += mid_in[other]
-
-    def add_edge(other):
-        for c in range(chunks):
-            edge_total(other, c, other).wait_recv()
-        before[0] += edge_in[other, 0]
-        before[J - 1] += edge_in[other, 1]
-
-    earlier(add_mid)
-    earlier(add_edge)
+    add_edges(chunks - 1)
 
     for c in range(chunks):
         both("lat", lambda side: lat_copy(STEPS - 1, side, c).wait_send())
         later(lambda other: edge_total(other, c).wait_send())
-        edge_end(0, c).wait()
-        edge_end(1, c).wait()
     later(lambda other: mid_total(other).wait_send())
-    mid_end().wait()
-
-
-def totals_kernel(scale, x, before, totals, end):
-    def row(i, total):
-        value = x[0, i]
-        total = total + value
-        totals[0, i] = total * scale
-        end[0, i] = value
-        return total
-
-    lax.fori_loop(0, x.shape[1], row, before[0], unroll=4)
+
+
+def totals_kernel(scale, x, before, totals, end, sums, end_sem, sums_sem):
+    J, I = x.shape[:2]
+
+    def out(which, j):
+        src, dst, sem = ((x, end, end_sem), (sums, totals, sums_sem))[which]
+        return pltpu.make_async_copy(src.at[j], dst.at[j], sem.at[j])
+
+    for j in range(J):
+        out(0, j).start()
+
+    @pl.loop(0, J)
+    def _(j):
+        def row(i, total):
+            total = total + x[j, i]
+            sums[j, i] = total * scale
+            return total
+
+        lax.fori_loop(0, I, row, before[j], unroll=4)
+        out(1, j).start()
+
+    for j in range(J):
+        out(0, j).wait()
+        out(1, j).wait()
 
 
 def per_device(sizes, initial_state, scaled_diffusivity, scaled_forcing):
@@ -346,14 +351,12 @@
     vmem = lambda *shape: pltpu.VMEM(shape, f32)
     sem = lambda *shape: pltpu.SemaphoreType.DMA(shape)
     hbm = pl.BlockSpec(memory_space=pltpu.HBM)
+    local = pl.BlockSpec(memory_space=pltpu.VMEM)
     end, before = pl.pallas_call(
         functools.partial(steps_kernel, sizes),
-        out_shape=(
-            jax.ShapeDtypeStruct((J, I, K, M), f32),
-            jax.ShapeDtypeStruct((J, K, M), f32),
-        ),
+        out_shape=(vmem(J, I, K, M), vmem(J, K, M)),
         in_specs=[hbm] * 3,
-        out_specs=(hbm, pl.BlockSpec(memory_space=pltpu.VMEM)),
+        out_specs=(local, local),
         scratch_shapes=[
             vmem(2, J + 2, I + 2, K + 2 * PAD, M),
             vmem(J, I, K, M),
@@ -371,24 +374,22 @@
             sem(2, 2),
             sem(2, 2),
             sem(3, J),
-            sem(3, chunks),
             sem(n_lon, chunks + 1),
             sem(n_lon, chunks + 1),
         ],
         compiler_params=pltpu.CompilerParams(
-            collective_id=0, has_side_effects=True, vmem_limit_bytes=58 * 2**20
+            collective_id=0, has_side_effects=True, vmem_limit_bytes=48 * 2**20
         ),
         name="steps",
     )(initial_state, scaled_diffusivity, scaled_forcing)
 
-    half = K // 2
-    block = pl.BlockSpec((1, I, half, M), lambda j, k: (j, 0, k, 0))
     return pl.pallas_call(
         functools.partial(totals_kernel, 1.0 / (I * n_lon)),
-        grid=(J, K // half),
         out_shape=(jax.ShapeDtypeStruct((J, I, K, M), f32),) * 2,
-        in_specs=[block, pl.BlockSpec((1, half, M), lambda j, k: (j, k, 0))],
-        out_specs=(block, block),
+        in_specs=[local, local],
+        out_specs=(hbm, hbm),
+        scratch_shapes=[vmem(J, I, K, M), sem(J), sem(J)],
+        compiler_params=pltpu.CompilerParams(vmem_limit_bytes=20 * 2**20),
         name="totals",
     )(end, before)
 

time: 115 us -> 106 us (0.922)
  Pallas kernels: 114 us -> 105 us
    pallas_call x2, Pallas kernels: 114 us -> 105 us  [the longest x1 98.9 us: per_device(): pl.pallas_call(functools.partial(steps_kernel, sizes), out_shape=(vmem(J,...]
where the time goes in v2:
time: 106 us; the launch traced here: 105 us
  Pallas kernels  105 us (99%)
    pallas_call x1, Pallas kernels, per_device(): pl.pallas_call(functools.partial(steps_kernel, sizes), out_shape=(vmem(J,...  98.9 us
    pallas_call x1, Pallas kernels, per_device(): pl.pallas_call(functools.partial(totals_kernel, 1.0 / (I * n_lon)), out_s...  5.96 us

profile of v2, /device:TPU:0, one launch (start us, length us, event | category | flops | bytes accessed | tf_op | source)
XLA Modules:
  0.0 105.5 jit_solution(1171549736753069889)
XLA Ops:
  0.6 98.9 %steps.1 = (f32[8,32,64,128]{3,2,1,0:T(8,128)S(1)}, f32[8,64,128]{2,1,0:T(8,128)S(1)}) custom-call(f32[8,32,64,128]{3,2,1,0:T(8,128)} %x.1, f32[8,32,64,128]{3,2,1,0:T(8,128)} %d.1, f32[8,32,64,128]{3,2,1,0:T(8,128)} %f.1), custom_call_target="tpu_custom_call" | custom-call | tf_op jit(solution)/shard_map/steps/pallas_call | solution.py:355
  99.5 6.0 %totals.1 = (f32[8,32,64,128]{3,2,1,0:T(8,128)}, f32[8,32,64,128]{3,2,1,0:T(8,128)}) custom-call(f32[8,32,64,128]{3,2,1,0:T(8,128)S(1)} %get-tuple-element.4.x, f32[8,64,128]{2,1,0:T(8,128)S(1)} %get-tuple-element.5.before), custom_call_target="tpu_custom_call" | custom-call | tf_op jit(solution)/shard_map/totals/pallas_call | solution.py:386
